TPU v7x, 32 devices: a whole 2x2x4 slice. The times are simulated.
32 devices in a mesh: group: 2 (over y), ctx: 4 (over z), head: 4 (over x, core).
Axes of the slice: x: 2, y: 2, z: 4, core: 2. Of those that a mesh axis runs over, the one named last changes fastest.
Arguments:
- query_nope: bfloat16 [512, 8192], P(('group', 'ctx'), 'head'), parts along dimension 0, may hold values from -6 to 6
- query_rope: bfloat16 [512, 4096], P(('group', 'ctx'), 'head'), parts along dimension 0, may hold values from -16 to 16
- kv_latent: bfloat16 [512, 512], P(('group', 'ctx'), 'head'), parts along dimension 0, may hold values from -1300 to 1300
- key_rope: bfloat16 [512, 64], P(('group', 'ctx')), parts along dimension 0, may hold values from -16 to 16
- latent_gain: float32 [512], replicated, may hold values from 0.1 to 1.9
- w_key: bfloat16 [512, 8192], P(None, 'head'), may hold values from -0.25 to 0.25
- w_value: bfloat16 [512, 8192], P(None, 'head'), may hold values from -0.25 to 0.25
- block_order: int32 [16], P('group'), parts along dimension 0, may hold values from 0 to 7, as said below
Outputs:
- attention_out: bfloat16 [512, 8192], P(('group', 'ctx'), 'head'), parts along dimension 0
There are 2 independent parts, one for each index of `group`. A program takes and returns all parts, laid end to end along the dimension named above; an argument that names none is the same for every part. Nothing has to cross between parts.
Inputs may be any that keep to these rules, and one draw needn't show every extreme that they name: `block_order`: A permutation of 0 to 7. Entries 2 c and 2 c + 1, for each c < 4, add up to 7.
All inputs are finite; a program needn't handle non-finite values.
Results may differ from a plain program's by a relative error of at most 0.0081.
Values may be sent and summed in bfloat16 or wider, within the bound.
A program may use at most 64 MiB of HBM per device.

v0:
```python
from functools import partial
import math

import jax
import jax.numpy as jnp
from jax import lax
from jax.sharding import PartitionSpec as P

ROPE = 64
NOPE = 128
VALUE_DIM = 128


EPSILON = 1e-06
NEGATIVE = -1e30


def rope_angle(positions, width):
    half_width = width // 2
    frequency = jnp.exp(-jnp.log(10000.0) * jnp.arange(half_width, dtype=jnp.float32) / half_width)
    return positions.astype(jnp.float32)[:, None] * frequency[None, :]


def rotate_pairs(values, angle):
    half_width = values.shape[-1] // 2
    first_half = values[..., :half_width]
    second = values[..., half_width:]
    cosine = jnp.cos(angle)
    sine_part = jnp.sin(angle)
    return jnp.concatenate(
        [first_half * cosine - second * sine_part, second * cosine + first_half * sine_part], -1
    )


def block_positions(begin_row, row_count, table, block_rows):
    row_ids = begin_row + jnp.arange(row_count, dtype=jnp.int32)
    blocks = row_ids // block_rows
    slot_ids = jnp.arange(table.shape[0], dtype=jnp.int32)
    looked = jnp.sum(jnp.where(blocks[:, None] == slot_ids[None, :], table[None, :], 0), axis=1)
    return looked * block_rows + row_ids % block_rows


def block_length(row_count, shard_rows):
    best_rows = shard_rows
    for factor in range(1, row_count // shard_rows + 1):
        if row_count // shard_rows % factor == 0 and shard_rows * factor <= max(512, shard_rows):
            best_rows = shard_rows * factor
    return best_rows


def attend_block(
    carried,
    query_latent,
    query_rotated,
    query_place,
    key_latent,
    key_rotated,
    key_place,
    score_scale,
):
    running_max, running_total, summed = carried
    contract = (((1,), (1,)), ((), ()))
    scores = lax.dot_general(query_latent, key_latent, contract, preferred_element_type=jnp.float32)
    scores = (
        scores
        + lax.dot_general(query_rotated, key_rotated, contract, preferred_element_type=jnp.float32)
    ) * score_scale
    visible = key_place[None, :] <= query_place[:, None]
    scores = jnp.where(visible, scores, NEGATIVE)
    new_max = jnp.maximum(running_max, jnp.max(scores, axis=1))
    exps = jnp.where(visible, jnp.exp(scores - new_max[:, None]), 0.0)
    shrink = jnp.exp(running_max - new_max)
    running_total = running_total * shrink + jnp.sum(exps, axis=1)
    summed = summed * shrink[:, None] + jnp.dot(
        exps.astype(jnp.bfloat16), key_latent, preferred_element_type=jnp.float32
    )
    return (new_max, running_total, summed)


def per_device(
    query_nope, query_rope, kv_latent, key_rope, latent_gain, w_key, w_value, block_order
):
    tokens_here = query_nope.shape[0]
    heads_here = w_key.shape[1] // NOPE
    latent_width = w_key.shape[0]
    block_rows = tokens_here // 2
    score_scale = 1.0 / math.sqrt(NOPE + ROPE)
    first_row = lax.axis_index("ctx") * tokens_here
    query_place = block_positions(first_row, tokens_here, block_order, block_rows)
    query_angle = rope_angle(query_place, ROPE)
    query_rotated = rotate_pairs(
        query_rope.astype(jnp.float32).reshape(tokens_here, heads_here, ROPE),
        query_angle[:, None, :],
    )
    query_rotated = query_rotated.astype(jnp.bfloat16).reshape(tokens_here * heads_here, ROPE)
    absorbed = jnp.einsum(
        "thd,lhd->thl",
        query_nope.reshape(tokens_here, heads_here, NOPE),
        w_key.reshape(latent_width, heads_here, NOPE),
        preferred_element_type=jnp.float32,
    )
    absorbed = absorbed.astype(jnp.bfloat16).reshape(tokens_here * heads_here, latent_width)
    row_place = jnp.repeat(query_place, heads_here)
    groups = ((absorbed, query_rotated, row_place),)
    initial = tuple(
        (
            (
                jnp.full((member[0].shape[0],), NEGATIVE, jnp.float32),
                jnp.zeros((member[0].shape[0],), jnp.float32),
                jnp.zeros((member[0].shape[0], latent_width), jnp.float32),
            )
            for member in groups
        )
    )
    columns = kv_latent.shape[1]
    column_part = kv_latent.astype(jnp.float32)
    square = lax.psum(jnp.sum(column_part * column_part, axis=1), "head")
    gain_part = lax.dynamic_slice_in_dim(latent_gain, lax.axis_index("head") * columns, columns, 0)
    scaled = (
        column_part * lax.rsqrt(square / latent_width + EPSILON)[:, None] * gain_part[None, :]
    ).astype(jnp.bfloat16)
    normed = lax.all_gather(scaled, "head", axis=1, tiled=True)
    key_rotated = rotate_pairs(key_rope.astype(jnp.float32), query_angle).astype(jnp.bfloat16)
    key_latent = lax.all_gather(normed, "ctx", axis=0, tiled=True)
    make_key_rotated = lax.all_gather(key_rotated, "ctx", axis=0, tiled=True)
    row_count = key_latent.shape[0]
    length = block_length(row_count, tokens_here)
    block_count = row_count // length
    latent_blocks = key_latent.reshape(block_count, length, latent_width)
    rotated_blocks = make_key_rotated.reshape(block_count, length, ROPE)
    block_starts = length * jnp.arange(block_count, dtype=jnp.int32)

    def one_block(state_now, operands):
        latent_block, rotated_block, first_key = operands
        key_place = block_positions(first_key, length, block_order, block_rows)
        updated = []
        for member, member_state in zip(groups, state_now):
            advance = partial(
                attend_block,
                query_latent=member[0],
                query_rotated=member[1],
                query_place=member[2],
                key_latent=latent_block,
                key_rotated=rotated_block,
                key_place=key_place,
                score_scale=score_scale,
            )
            updated.append(advance(member_state))
        return (tuple(updated), None)

    result, unused = lax.scan(one_block, initial, (latent_blocks, rotated_blocks, block_starts))
    mixed = jnp.concatenate(
        [
            (member_state[2] / member_state[1][:, None]).astype(jnp.bfloat16)
            for member_state in result
        ],
        0,
    )
    mixed = mixed.reshape(tokens_here, heads_here, latent_width)
    output = jnp.einsum(
        "thl,lhe->the",
        mixed,
        w_value.reshape(latent_width, heads_here, VALUE_DIM),
        preferred_element_type=jnp.float32,
    )
    return output.astype(jnp.bfloat16).reshape(tokens_here, heads_here * VALUE_DIM)


def solution(mesh):
    return jax.shard_map(
        per_device,
        mesh=mesh,
        in_specs=(
            P(("group", "ctx"), "head"),
            P(("group", "ctx"), "head"),
            P(("group", "ctx"), "head"),
            P(("group", "ctx"), None),
            P(),
            P(None, "head"),
            P(None, "head"),
            P("group"),
        ),
        out_specs=P(("group", "ctx"), "head"),
        check_vma=False,
    )
```

profile of v0, /device:TPU:0, one launch (start us, length us, event | category | flops | bytes accessed | tf_op | source)
XLA Modules:
  0.0 54.3 jit_solution(1356977436039085521)
XLA Ops:
  0.0 0.0 copy-start
  0.0 0.9 %dynamic_slice.12 = f32[128]{0:T(128)S(1)} dynamic-slice(f32[512]{0:T(512)} %param.12, s32[]{:T(128)S(6)} %select_n.69), dynamic_slice_sizes={128} | dynamic-slice | bytes 1028 | tf_op jit(solution)/shard_map/dynamic_slice | solution.py:118
  0.9 0.8 %fusion.33 = f32[64]{0:T(128)S(1)} fusion(bf16[64,128]{1,0:T(8,128)(2,1)} %param.10), kind=kLoop, calls=%fused_computation.34 | loop fusion | flops 24512 | bytes 16640 | tf_op jit(solution)/shard_map/reduce_sum | solution.py:117
  1.7 8.4 %psum.7 = f32[64]{0:T(128)S(1)} all-reduce(f32[64]{0:T(128)S(1)} %fusion.33), channel_id=1, replica_groups=mesh['group'=2,'ctx'=4,'head'=4] {'head'}, use_global_device_ids=true, to_apply=%region_3.4 | all-reduce | flops 64 | bytes 512 | tf_op jit(solution)/shard_map/psum | solution.py:117
  10.1 0.8 %fusion.35 = bf16[64,128]{1,0:T(8,128)(2,1)S(1)} fusion(bf16[64,128]{1,0:T(8,128)(2,1)} %param.10, f32[128]{0:T(128)S(1)} %dynamic_slice.12, f32[64]{0:T(128)S(1)} %add_rsqrt_fusion), kind=kLoop, calls=%fused_computation.36 | loop fusion | flops 32768 | bytes 33536 | tf_op jit(solution)/shard_map/convert_element_type | solution.py:121
  10.9 5.3 %all_gather.9 = bf16[64,512]{1,0:T(8,128)(2,1)S(1)} all-gather(bf16[64,128]{1,0:T(8,128)(2,1)S(1)} %fusion.35), channel_id=1, replica_groups=mesh['group'=2,'ctx'=4,'head'=4] {'head'}, dimensions={1}, use_global_device_ids=true | all-gather | bytes 81920 | tf_op jit(solution)/shard_map/all_gather | solution.py:122
  16.2 14.1 %all_gather.10 = bf16[256,512]{1,0:T(8,128)(2,1)S(1)} all-gather(bf16[64,512]{1,0:T(8,128)(2,1)S(1)} %all_gather.9), channel_id=1, replica_groups=mesh['group'=2,'ctx'=4,'head'=4] {'ctx'}, dimensions={0}, use_global_device_ids=true | all-gather | bytes 327680 | tf_op jit(solution)/shard_map/all_gather | solution.py:124
  30.2 0.0 copy-done
  30.2 1.8 %fusion.9 = bf16[64,16,512]{2,0,1:T(8,128)(2,1)S(1)} fusion(bf16[512,2048]{1,0:T(8,128)(2,1)S(1)} %copy-done, bf16[64,2048]{1,0:T(8,128)(2,1)} %param.8), kind=kOutput, calls=%fused_computation.8 | convolution fusion | flops 134742016 | bytes 3407872 | tf_op jit(solution)/shard_map/thd,lhd->thl/dot_general | solution.py:96
  32.0 0.0 copy-start.3
  32.1 0.0 copy-start.2
  32.1 0.0 copy-start.1
  32.1 0.6 %copy.21 = bf16[64,16,512]{2,1,0:T(8,128)(2,1)S(1)} copy(bf16[64,16,512]{2,0,1:T(8,128)(2,1)S(1)} %fusion.9) | data formatting | bytes 2097152 | tf_op jit(solution)/shard_map/convert_element_type | solution.py:102
  32.7 1.5 %fusion.46 = f32[1024,256]{0,1:T(8,128)} fusion(bf16[1024,512]{1,0:T(8,128)(2,1)S(1)} %bitcast.45, bf16[256,512]{1,0:T(8,128)(2,1)S(1)} %all_gather.10), kind=kOutput, calls=%fused_computation.68 | convolution fusion | flops 268435456 | bytes 2359296 | tf_op jit(solution)/shard_map/while/body/eval_jaxpr/dot_general | solution.py:63
  34.1 0.0 copy-done.3
  34.2 0.1 select_reduce_fusion.1
  34.3 0.0 copy-done.2
  34.3 0.2 multiply_cosine_fusion
  34.5 0.1 pad_maximum_fusion
  34.6 13.3 %all_gather.11 = bf16[256,64]{1,0:T(8,128)(2,1)S(1)} all-gather(bf16[64,64]{1,0:T(8,128)(2,1)S(1)} %pad_maximum_fusion), channel_id=1, replica_groups=mesh['group'=2,'ctx'=4,'head'=4] {'ctx'}, dimensions={0}, use_global_device_ids=true | all-gather | bytes 40960 | tf_op jit(solution)/shard_map/all_gather | solution.py:125
  47.9 0.0 copy-done.1
  47.9 0.1 reshape.178
  48.0 0.2 subtract_convert_fusion
  48.2 0.1 broadcast_in_dim.74
  48.3 0.1 le.23
  48.4 0.1 select_reduce_fusion
  48.5 1.7 %fusion.45 = (f32[1024]{0:T(1024)S(1)}, f32[1024,256]{0,1:T(8,128)S(1)}) fusion(f32[1024,256]{0,1:T(8,128)} %fusion.46, bf16[256,64]{1,0:T(8,128)(2,1)S(1)} %all_gather.11, bf16[1024,32]{1,0:T(8,128)(2,1)S(1)} %bitcast.47, bf16[1024,32]{1,0:T(8,128)(2,1)S(1)} %bitcast.46, s32[1024]{0:T(1024)S(1)} %le.23, s32[256]{0:T(256)S(1)} %fusion.38), kind=kOutput, calls=%fused_computation.67 | convolution fusion | flops 35126272 | bytes 2270208 | tf_op jit(solution)/shard_map/while/body/eval_jaxpr/dot_general | solution.py:66
  50.2 0.2 fusion.21
  50.4 0.0 copy-start.4
  50.4 0.6 %divide_convert_fusion = bf16[1024,512]{1,0:T(8,128)(2,1)S(1)} fusion(bf16[256,512]{1,0:T(8,128)(2,1)S(1)} %all_gather.10, f32[1024]{0:T(1024)S(1)} %get-tuple-element.40, f32[1024]{0:T(1024)S(1)} %get-tuple-element.29, f32[1024,256]{0,1:T(8,128)S(1)} %get-tuple-element.48, f32[1024]{0:T(1024)S(1)} %broadcast_maximum_fusion, s32[1024]{0:T(1024)S(1)} %le.23, ...), kind=kOutput, calls=%fused_computation.6 | convolution fusion | flops 271056896 | bytes 2376704 | tf_op jit(solution)/shard_map/while/body/eval_jaxpr/dot_general | solution.py:74
  51.0 1.0 %copy-done.4 = bf16[512,2048]{1,0:T(8,128)(2,1)S(1)} copy-done((bf16[512,2048]{1,0:T(8,128)(2,1)S(1)}, bf16[512,2048]{1,0:T(8,128)(2,1)}, u32[]{:S(2)}) %copy-start.4) | copy-done | bytes 2097176
  52.0 1.5 %fusion.17 = bf16[16,8,8,128]{3,2,1,0:T(8,128)(2,1)S(1)} fusion(bf16[64,16,512]{2,1,0:T(8,128)(2,1)S(1)} %bitcast.48, bf16[512,2048]{1,0:T(8,128)(2,1)S(1)} %copy-done.4), kind=kOutput, calls=%fused_computation.14 | convolution fusion | flops 134348800 | bytes 3407872 | tf_op jit(solution)/shard_map/thl,lhe->the/dot_general | solution.py:160
  53.5 0.8 %copy.52 = bf16[16,8,8,128]{3,2,0,1:T(8,128)(2,1)} copy(bf16[16,8,8,128]{3,2,1,0:T(8,128)(2,1)S(1)} %fusion.17) | data formatting | bytes 524288 | tf_op jit(solution)/shard_map/reshape | solution.py:166
  (9 shorter events, 0.1 us)
Async XLA Ops:
  0.0 30.2 %copy-start = (bf16[512,2048]{1,0:T(8,128)(2,1)S(1)}, bf16[512,2048]{1,0:T(8,128)(2,1)}, u32[]{:S(2)}) copy-start(bf16[512,2048]{1,0:T(8,128)(2,1)} %param.13) | copy-start | bytes 6291460
  32.0 2.1 %copy-start.3 = (s32[8]{0:T(128)S(1)}, s32[8]{0:T(128)}, u32[]{:S(2)}) copy-start(s32[8]{0:T(128)} %param.15) | copy-start | bytes 100
  32.1 2.2 %copy-start.2 = (bf16[64,64]{1,0:T(8,128)(2,1)S(1)}, bf16[64,64]{1,0:T(8,128)(2,1)}, u32[]{:S(2)}) copy-start(bf16[64,64]{1,0:T(8,128)(2,1)} %param.11) | copy-start | bytes 24580
  32.1 15.8 %copy-start.1 = (bf16[64,1024]{1,0:T(8,128)(2,1)S(1)}, bf16[64,1024]{1,0:T(8,128)(2,1)}, u32[]{:S(2)}) copy-start(bf16[64,1024]{1,0:T(8,128)(2,1)} %param.9) | copy-start | bytes 393220
  50.4 1.6 %copy-start.4 = (bf16[512,2048]{1,0:T(8,128)(2,1)S(1)}, bf16[512,2048]{1,0:T(8,128)(2,1)}, u32[]{:S(2)}) copy-start(bf16[512,2048]{1,0:T(8,128)(2,1)} %param.14) | copy-start | bytes 6291460
where the time goes:
time: 54.7 us; the launch traced here: 54.3 us
  blocking collectives  41 us (75%)
  matrix products  7 us (13%)
  local copies, waits for them, and re-layouts  3.53 us (6%)
  other arithmetic  2.6 us (5%)
    all_gather x1, blocking collectives, per_device(): key_latent = lax.all_gather(normed, 'ctx', axis=0, tiled=True)  14.1 us
    all_gather x1, blocking collectives, per_device(): make_key_rotated = lax.all_gather(key_rotated, 'ctx', axis=0, tiled=True)  13.3 us
    psum x1, blocking collectives, per_device(): square = lax.psum(jnp.sum(column_part * column_part, axis=1), 'head')  8.37 us
    all_gather x1, blocking collectives, per_device(): normed = lax.all_gather(scaled, 'head', axis=1, tiled=True)  5.25 us
    dot_general x1, matrix products, per_device(): jnp.einsum('thd,lhd->thl', query_nope.reshape(tokens_here, heads_here, NO...  1.79 us
    dot_general x1, matrix products, attend_block(): lax.dot_general(query_rotated, key_rotated, contract, preferred_element_t...  1.65 us
    dot_general x1, matrix products, per_device(): jnp.einsum('thl,lhe->the', mixed, w_value.reshape(latent_width, heads_her...  1.49 us
    dot_general x1, matrix products, attend_block(): lax.dot_general(query_latent, key_latent, contract, preferred_element_typ...  1.46 us

commit v1 on v0

--- a/solution.py
+++ b/solution.py
@@ -4,6 +4,8 @@
 import jax
 import jax.numpy as jnp
 from jax import lax
+from jax.experimental import pallas as pl
+from jax.experimental.pallas import tpu as pltpu
 from jax.sharding import PartitionSpec as P
 
 ROPE = 64
@@ -166,9 +168,381 @@
     return output.astype(jnp.bfloat16).reshape(tokens_here, heads_here * VALUE_DIM)
 
 
+LANES = 128
+FUSED_ROWS = 512
+HEAD_GROUP = 4
+MESH = pl.DeviceIdType.MESH
+
+
+def flip(index, stride):
+    return index + stride - 2 * stride * ((index // stride) % 2)
+
+
+def strides_of(count):
+    strides = []
+    stride = count // 2
+    while stride >= 1:
+        strides.append(stride)
+        stride //= 2
+    return strides
+
+
+def lane_frequency(lanes):
+    half = ROPE // 2
+    rest = lanes % half
+    frequency = jnp.ones(lanes.shape, jnp.float32)
+    bit = 1
+    while bit < half:
+        frequency = frequency * jnp.where((rest // bit) % 2 == 1, 10000.0 ** (-bit / half), 1.0)
+        bit *= 2
+    return frequency
+
+
+def turn(values, cosine, signed_sine, first_lanes):
+    half = ROPE // 2
+    ahead = pltpu.roll(values, LANES - half, 1)
+    behind = pltpu.roll(values, half, 1)
+    return values * cosine + jnp.where(first_lanes, ahead, behind) * signed_sine
+
+
+def fused_kernel(
+    contexts,
+    shards,
+    order_ref,
+    gain_ref,
+    nope_hbm,
+    rope_hbm,
+    latent_hbm,
+    key_rope_hbm,
+    w_key_hbm,
+    w_value_hbm,
+    out_hbm,
+    nope,
+    rope,
+    w_key,
+    w_value,
+    latents,
+    ropes,
+    queries,
+    keys,
+    outs,
+    load_sem,
+    key_sem,
+    own_sem,
+    out_sem,
+    latent_send,
+    latent_recv,
+    rope_send,
+    rope_recv,
+):
+    group = lax.axis_index("group")
+    ctx = lax.axis_index("ctx")
+    shard = lax.axis_index("head")
+    tokens = nope.shape[0]
+    heads = nope.shape[1] // NOPE
+    latent_width = w_key.shape[0]
+    block_rows = tokens // 2
+    blocks = 2 * contexts
+    rope_rows = ropes.shape[2]
+    chunks = key_sem.shape[0]
+    chunk = w_key.shape[1] // chunks
+
+    own_latent = pltpu.make_async_copy(latent_hbm, latents.at[ctx, shard], own_sem.at[0])
+    own_rope = pltpu.make_async_copy(
+        key_rope_hbm.at[pl.ds(pl.multiple_of(shard * rope_rows, rope_rows), rope_rows), :],
+        ropes.at[ctx, shard],
+        own_sem.at[1],
+    )
+    own_latent.start()
+    own_rope.start()
+    load_nope = pltpu.make_async_copy(nope_hbm, nope, load_sem.at[0])
+    load_rope = pltpu.make_async_copy(rope_hbm, rope, load_sem.at[1])
+    load_value = pltpu.make_async_copy(w_value_hbm, w_value, load_sem.at[2])
+    load_nope.start()
+    load_keys = []
+    for part in range(chunks):
+        columns = pl.ds(part * chunk, chunk)
+        load = pltpu.make_async_copy(w_key_hbm.at[:, columns], w_key.at[:, columns], key_sem.at[part])
+        load.start()
+        load_keys.append(load)
+    load_rope.start()
+    load_value.start()
+
+    peers = [(group, flip_all(ctx, step), shard) for step in range(1, contexts)]
+    strides = strides_of(shards)
+    partners = [(group, ctx, flip(shard, stride)) for stride in strides]
+    barrier = pltpu.get_barrier_semaphore()
+    for device in peers + partners:
+        pl.semaphore_signal(barrier, inc=1, device_id=device, device_id_type=MESH)
+    pl.semaphore_wait(barrier, len(peers) + len(partners))
+
+    own_latent.wait()
+    own_rope.wait()
+    sent = []
+
+    def send(slot, index, target):
+        place, part = slot
+        for buffer, send_sem, recv_sem in (
+            (latents, latent_send, latent_recv),
+            (ropes, rope_send, rope_recv),
+        ):
+            copy = pltpu.make_async_remote_copy(
+                src_ref=buffer.at[place, part],
+                dst_ref=buffer.at[place, part],
+                send_sem=send_sem.at[index],
+                recv_sem=recv_sem.at[place, part],
+                device_id=target,
+                device_id_type=MESH,
+            )
+            copy.start()
+            sent.append(copy)
+
+    def arrive(place, part):
+        for buffer, send_sem, recv_sem in (
+            (latents, latent_send, latent_recv),
+            (ropes, rope_send, rope_recv),
+        ):
+            pltpu.make_async_remote_copy(
+                src_ref=buffer.at[place, part],
+                dst_ref=buffer.at[place, part],
+                send_sem=send_sem.at[0],
+                recv_sem=recv_sem.at[place, part],
+                device_id=partners[0] if partners else peers[0],
+                device_id_type=MESH,
+            ).wait_recv()
+
+    counter = [0]
+
+    def next_index():
+        counter[0] += 1
+        return counter[0] - 1
+
+    for target in peers:
+        send((ctx, shard), next_index(), target)
+    for target in partners:
+        send((ctx, shard), next_index(), target)
+
+    def absorb(part):
+        load_keys[part].wait()
+        for head in range(part * heads // chunks, (part + 1) * heads // chunks):
+            columns = slice(head * NOPE, (head + 1) * NOPE)
+            absorbed = lax.dot_general(
+                nope[:, columns],
+                w_key[:, columns],
+                (((1,), (1,)), ((), ())),
+                preferred_element_type=jnp.float32,
+            )
+            queries[head * tokens : (head + 1) * tokens, :latent_width] = absorbed.astype(jnp.bfloat16)
+
+    load_nope.wait()
+    absorb(0)
+
+    lanes = lax.broadcasted_iota(jnp.int32, (1, LANES), 1)
+    frequency = lane_frequency(lanes)
+    first_lanes = lanes % ROPE < ROPE // 2
+    sign = jnp.where(first_lanes, -1.0, 1.0)
+    table_rows = -(-(blocks + 2) // 8) * 8
+    row_ids = lax.broadcasted_iota(jnp.int32, (table_rows, LANES), 0)
+    base = jnp.zeros((table_rows, LANES), jnp.int32)
+    slots = [order_ref[slot] for slot in range(blocks)] + [order_ref[2 * ctx], order_ref[2 * ctx + 1]]
+    for row, slot in enumerate(slots):
+        base = jnp.where(row_ids == row, slot * block_rows, base)
+    base_angle = base.astype(jnp.float32) * frequency
+    step_angle = (
+        lax.broadcasted_iota(jnp.int32, (block_rows, LANES), 0).astype(jnp.float32) * frequency
+    )
+    base_cos, base_sin = jnp.cos(base_angle), jnp.sin(base_angle)
+    step_cos, step_sin = jnp.cos(step_angle), jnp.sin(step_angle)
+
+    def tables(first, second):
+        cosines, sines = [], []
+        for row in (first, second):
+            one_cos, one_sin = base_cos[row : row + 1], base_sin[row : row + 1]
+            cosines.append(one_cos * step_cos - one_sin * step_sin)
+            sines.append((one_sin * step_cos + one_cos * step_sin) * sign)
+        return jnp.concatenate(cosines, 0), jnp.concatenate(sines, 0)
+
+    query_cos, query_sin = tables(blocks, blocks + 1)
+    per_tile = LANES // ROPE
+    load_rope.wait()
+    for tile in range(heads // per_tile):
+        turned = turn(
+            rope[:, tile * LANES : (tile + 1) * LANES].astype(jnp.float32),
+            query_cos,
+            query_sin,
+            first_lanes,
+        )
+        for inner in range(per_tile):
+            head = tile * per_tile + inner
+            queries[head * tokens : (head + 1) * tokens, latent_width:] = jnp.where(
+                lanes // ROPE == inner, turned, 0.0
+            ).astype(jnp.bfloat16)
+
+    steps = list(range(1, contexts))
+    for order, step in enumerate(steps):
+        if order + 1 < chunks:
+            absorb(order + 1)
+        place = flip_all(ctx, step)
+        arrive(place, shard)
+        for target in partners:
+            send((place, shard), next_index(), target)
+    for part in range(len(steps) + 1, chunks):
+        absorb(part)
+
+    held = [shard]
+    for level, stride in enumerate(strides):
+        fresh = [flip(part, stride) for part in held]
+        for step in range(contexts):
+            place = ctx if step == 0 else flip_all(ctx, step)
+            for part in fresh:
+                arrive(place, part)
+                for target in partners[level + 1 :]:
+                    send((place, part), next_index(), target)
+        held = held + fresh
+
+    gain = gain_ref[...]
+    for place in range(contexts):
+        raw = jnp.concatenate([latents[place, part] for part in range(shards)], 1).astype(jnp.float32)
+        mean = jnp.sum(raw * raw, axis=1, keepdims=True) / latent_width
+        normed = raw * lax.rsqrt(mean + EPSILON) * gain
+        rows = slice(place * tokens, (place + 1) * tokens)
+        keys[rows, :latent_width] = normed.astype(jnp.bfloat16)
+        key_raw = jnp.concatenate([ropes[place, part] for part in range(shards)], 0).astype(jnp.float32)
+        key_raw = jnp.concatenate([key_raw] * per_tile, 1)
+        key_cos, key_sin = tables(2 * place, 2 * place + 1)
+        keys[rows, latent_width:] = turn(key_raw, key_cos, key_sin, first_lanes).astype(jnp.bfloat16)
+
+    total_rows = contexts * tokens
+    key_ids = lax.broadcasted_iota(jnp.int32, (1, total_rows), 1)
+    key_base = jnp.zeros((1, total_rows), jnp.int32)
+    for row in range(blocks):
+        key_base = jnp.where(key_ids // block_rows == row, slots[row], key_base)
+    key_place = key_base * block_rows + key_ids % block_rows
+    query_ids = lax.broadcasted_iota(jnp.int32, (HEAD_GROUP * tokens, 1), 0) % tokens
+    query_place = (
+        jnp.where(query_ids // block_rows == 0, slots[blocks], slots[blocks + 1]) * block_rows
+        + query_ids % block_rows
+    )
+    visible = key_place <= query_place
+    exponent = math.log2(math.e) / math.sqrt(NOPE + ROPE)
+
+    load_value.wait()
+    stores = []
+    for cluster in range(heads // HEAD_GROUP):
+        rows = slice(cluster * HEAD_GROUP * tokens, (cluster + 1) * HEAD_GROUP * tokens)
+        scores = lax.dot_general(
+            queries[rows, :], keys[...], (((1,), (1,)), ((), ())), preferred_element_type=jnp.float32
+        )
+        scores = jnp.where(visible, scores, NEGATIVE)
+        top = jnp.max(scores, axis=1, keepdims=True)
+        exps = jnp.exp2((scores - top) * exponent)
+        total = jnp.sum(exps, axis=1, keepdims=True)
+        mixed = jnp.dot(
+            exps.astype(jnp.bfloat16), keys[:, :latent_width], preferred_element_type=jnp.float32
+        )
+        mixed = (mixed * (1.0 / total)).astype(jnp.bfloat16)
+        for inner in range(HEAD_GROUP):
+            head = cluster * HEAD_GROUP + inner
+            columns = slice(head * VALUE_DIM, (head + 1) * VALUE_DIM)
+            outs[:, columns] = jnp.dot(
+                mixed[inner * tokens : (inner + 1) * tokens],
+                w_value[:, columns],
+                preferred_element_type=jnp.float32,
+            ).astype(jnp.bfloat16)
+        columns = pl.ds(cluster * HEAD_GROUP * VALUE_DIM, HEAD_GROUP * VALUE_DIM)
+        store = pltpu.make_async_copy(outs.at[:, columns], out_hbm.at[:, columns], out_sem.at[cluster])
+        store.start()
+        stores.append(store)
+    for store in stores:
+        store.wait()
+    for copy in sent:
+        copy.wait_send()
+
+
+def flip_all(index, step):
+    result = index
+    bit = 1
+    while bit <= step:
+        if (step // bit) % 2 == 1:
+            result = flip(result, bit)
+        bit *= 2
+    return result
+
+
+def fused_device(
+    contexts,
+    shards,
+    query_nope,
+    query_rope,
+    kv_latent,
+    key_rope,
+    latent_gain,
+    w_key,
+    w_value,
+    block_order,
+):
+    tokens, nope_width = query_nope.shape
+    heads = nope_width // NOPE
+    latent_width = w_key.shape[0]
+    rope_rows = tokens // shards
+    sends = (contexts - 1) + contexts * (shards - 1)
+    anywhere = pl.BlockSpec(memory_space=pl.ANY)
+    return pl.pallas_call(
+        partial(fused_kernel, contexts, shards),
+        out_shape=jax.ShapeDtypeStruct((tokens, heads * VALUE_DIM), jnp.bfloat16),
+        in_specs=[
+            pl.BlockSpec(memory_space=pltpu.SMEM),
+            pl.BlockSpec(memory_space=pltpu.VMEM),
+        ]
+        + [anywhere] * 6,
+        out_specs=anywhere,
+        scratch_shapes=[
+            pltpu.VMEM(query_nope.shape, jnp.bfloat16),
+            pltpu.VMEM(query_rope.shape, jnp.bfloat16),
+            pltpu.VMEM(w_key.shape, jnp.bfloat16),
+            pltpu.VMEM(w_value.shape, jnp.bfloat16),
+            pltpu.VMEM((contexts, shards) + kv_latent.shape, jnp.bfloat16),
+            pltpu.VMEM((contexts, shards, rope_rows, ROPE), jnp.bfloat16),
+            pltpu.VMEM((heads * tokens, latent_width + LANES), jnp.bfloat16),
+            pltpu.VMEM((contexts * tokens, latent_width + LANES), jnp.bfloat16),
+            pltpu.VMEM((tokens, heads * VALUE_DIM), jnp.bfloat16),
+            pltpu.SemaphoreType.DMA((3,)),
+            pltpu.SemaphoreType.DMA((4,)),
+            pltpu.SemaphoreType.DMA((2,)),
+            pltpu.SemaphoreType.DMA((heads // HEAD_GROUP,)),
+            pltpu.SemaphoreType.DMA((sends,)),
+            pltpu.SemaphoreType.DMA((contexts, shards)),
+            pltpu.SemaphoreType.DMA((sends,)),
+            pltpu.SemaphoreType.DMA((contexts, shards)),
+        ],
+        compiler_params=pltpu.CompilerParams(collective_id=0, has_side_effects=True),
+    )(
+        block_order,
+        latent_gain.reshape(1, latent_width),
+        query_nope,
+        query_rope,
+        kv_latent,
+        key_rope,
+        w_key,
+        w_value,
+    )
+
+
+def power_of_two(count):
+    return count & (count - 1) == 0
+
+
 def solution(mesh):
+    contexts, shards = mesh.shape["ctx"], mesh.shape["head"]
+
+    def device_step(*arguments):
+        small = contexts * arguments[0].shape[0] <= FUSED_ROWS
+        if small and power_of_two(contexts) and power_of_two(shards):
+            return fused_device(contexts, shards, *arguments)
+        return per_device(*arguments)
+
     return jax.shard_map(
-        per_device,
+        device_step,
         mesh=mesh,
         in_specs=(
             P(("group", "ctx"), "head"),

time: 54.7 us -> 19.3 us (0.35)
  the two profiles are of different devices: /device:TPU:0 before, /device:TPU:1 now
where the time goes in v1:
time: 19.3 us; the launch traced here: 19.2 us
  Pallas kernels  17.5 us (91%)
  local copies, waits for them, and re-layouts  1.67 us (9%)
    pallas_call x1, Pallas kernels, fused_device(): pl.pallas_call(partial(fused_kernel, contexts, shards), out_shape=jax.Sha...  17.5 us
    unnamed x1, local copies, waits for them, and re-layouts  1.67 us

profile of v1, /device:TPU:1, one launch (start us, length us, event | category | flops | bytes accessed | tf_op | source)
XLA Modules:
  0.0 19.2 jit_solution(13935980914619566533)
XLA Ops:
  0.0 17.5 %shard_map.82 = bf16[64,2048]{1,0:T(8,128)(2,1)} custom-call(s32[8]{0:T(128)} %order_ref.1, f32[1,512]{1,0:T(1,128)} %bitcast.1, bf16[64,2048]{1,0:T(8,128)(2,1)} %nope_hbm.1, bf16[64,1024]{1,0:T(8,128)(2,1)} %rope_hbm.1, bf16[64,128]{1,0:T(8,128)(2,1)} %latent_hbm.1, bf16[64,64]{1,0:T(8,128)(2,1)} %key_rope_hbm.1, bf16[512,2048]{1,0:T(8,128)(2,1)} %w_key_hbm.1, ...), custom_call_target="tpu_custom_call" | custom-call | tf_op jit(solution)/shard_map/pallas_call | solution.py:490
  17.5 1.7 %copy.10 = bf16[64,2048]{1,0:T(8,128)(2,1)} copy(bf16[64,2048]{1,0:T(8,128)(2,1)} %shard_map.82) | data formatting | bytes 524288

commit v2 on v1

--- a/solution.py
+++ b/solution.py
@@ -171,6 +171,9 @@
 LANES = 128
 FUSED_ROWS = 512
 HEAD_GROUP = 4
+VMEM_BYTES = 67043328
+VMEM_SPARE = 2**17
+VMEM_GRANT = 24 * 2**20
 MESH = pl.DeviceIdType.MESH
 
 
@@ -208,28 +211,28 @@
 def fused_kernel(
     contexts,
     shards,
-    order_ref,
-    gain_ref,
+    order_hbm,
+    gain_hbm,
     nope_hbm,
     rope_hbm,
     latent_hbm,
     key_rope_hbm,
     w_key_hbm,
     w_value_hbm,
-    out_hbm,
+    queries,
+    keys,
+    bias,
+    w_value,
+    order_ref,
+    gain_ref,
     nope,
     rope,
     w_key,
-    w_value,
     latents,
     ropes,
-    queries,
-    keys,
-    outs,
     load_sem,
     key_sem,
     own_sem,
-    out_sem,
     latent_send,
     latent_recv,
     rope_send,
@@ -247,6 +250,12 @@
     chunks = key_sem.shape[0]
     chunk = w_key.shape[1] // chunks
 
+    peers = [(group, flip_all(ctx, step), shard) for step in range(contexts - 1, 0, -1)]
+    strides = strides_of(shards)
+    partners = [(group, ctx, flip(shard, stride)) for stride in strides]
+    barrier = pltpu.get_barrier_semaphore()
+    for device in peers + partners:
+        pl.semaphore_signal(barrier, inc=1, device_id=device, device_id_type=MESH)
     own_latent = pltpu.make_async_copy(latent_hbm, latents.at[ctx, shard], own_sem.at[0])
     own_rope = pltpu.make_async_copy(
         key_rope_hbm.at[pl.ds(pl.multiple_of(shard * rope_rows, rope_rows), rope_rows), :],
@@ -255,6 +264,8 @@
     )
     own_latent.start()
     own_rope.start()
+    load_order = pltpu.make_async_copy(order_hbm, order_ref, own_sem.at[2])
+    load_gain = pltpu.make_async_copy(gain_hbm, gain_ref, own_sem.at[3])
     load_nope = pltpu.make_async_copy(nope_hbm, nope, load_sem.at[0])
     load_rope = pltpu.make_async_copy(rope_hbm, rope, load_sem.at[1])
     load_value = pltpu.make_async_copy(w_value_hbm, w_value, load_sem.at[2])
@@ -266,14 +277,10 @@
         load.start()
         load_keys.append(load)
     load_rope.start()
+    load_order.start()
+    load_gain.start()
     load_value.start()
 
-    peers = [(group, flip_all(ctx, step), shard) for step in range(1, contexts)]
-    strides = strides_of(shards)
-    partners = [(group, ctx, flip(shard, stride)) for stride in strides]
-    barrier = pltpu.get_barrier_semaphore()
-    for device in peers + partners:
-        pl.semaphore_signal(barrier, inc=1, device_id=device, device_id_type=MESH)
     pl.semaphore_wait(barrier, len(peers) + len(partners))
 
     own_latent.wait()
@@ -336,6 +343,8 @@
 
     load_nope.wait()
     absorb(0)
+    load_order.wait()
+    load_gain.wait()
 
     lanes = lax.broadcasted_iota(jnp.int32, (1, LANES), 1)
     frequency = lane_frequency(lanes)
@@ -418,22 +427,30 @@
     for row in range(blocks):
         key_base = jnp.where(key_ids // block_rows == row, slots[row], key_base)
     key_place = key_base * block_rows + key_ids % block_rows
-    query_ids = lax.broadcasted_iota(jnp.int32, (HEAD_GROUP * tokens, 1), 0) % tokens
+    query_ids = lax.broadcasted_iota(jnp.int32, (tokens, 1), 0)
     query_place = (
         jnp.where(query_ids // block_rows == 0, slots[blocks], slots[blocks + 1]) * block_rows
         + query_ids % block_rows
     )
-    visible = key_place <= query_place
+    bias[...] = jnp.where(key_place <= query_place, 0.0, NEGATIVE)
+    load_value.wait()
+    for copy in sent:
+        copy.wait_send()
+
+
+def attend_kernel(queries, keys, bias, w_value, out_hbm, outs, out_sem):
+    tokens = bias.shape[0]
+    heads = queries.shape[0] // tokens
+    latent_width = w_value.shape[0]
     exponent = math.log2(math.e) / math.sqrt(NOPE + ROPE)
-
-    load_value.wait()
+    hidden = jnp.concatenate([bias[...]] * HEAD_GROUP, 0)
     stores = []
     for cluster in range(heads // HEAD_GROUP):
         rows = slice(cluster * HEAD_GROUP * tokens, (cluster + 1) * HEAD_GROUP * tokens)
         scores = lax.dot_general(
             queries[rows, :], keys[...], (((1,), (1,)), ((), ())), preferred_element_type=jnp.float32
         )
-        scores = jnp.where(visible, scores, NEGATIVE)
+        scores = scores + hidden
         top = jnp.max(scores, axis=1, keepdims=True)
         exps = jnp.exp2((scores - top) * exponent)
         total = jnp.sum(exps, axis=1, keepdims=True)
@@ -455,8 +472,6 @@
         stores.append(store)
     for store in stores:
         store.wait()
-    for copy in sent:
-        copy.wait_send()
 
 
 def flip_all(index, step):
@@ -487,35 +502,40 @@
     rope_rows = tokens // shards
     sends = (contexts - 1) + contexts * (shards - 1)
     anywhere = pl.BlockSpec(memory_space=pl.ANY)
-    return pl.pallas_call(
+    on_chip = pl.BlockSpec(memory_space=pltpu.VMEM)
+    rows = contexts * tokens
+    handed = 2 * (heads * tokens + rows) * (latent_width + LANES) + 4 * tokens * rows + 2 * w_value.size
+    prepared = pl.pallas_call(
         partial(fused_kernel, contexts, shards),
-        out_shape=jax.ShapeDtypeStruct((tokens, heads * VALUE_DIM), jnp.bfloat16),
-        in_specs=[
-            pl.BlockSpec(memory_space=pltpu.SMEM),
-            pl.BlockSpec(memory_space=pltpu.VMEM),
-        ]
-        + [anywhere] * 6,
-        out_specs=anywhere,
+        out_shape=[
+            pltpu.VMEM((heads * tokens, latent_width + LANES), jnp.bfloat16),
+            pltpu.VMEM((rows, latent_width + LANES), jnp.bfloat16),
+            pltpu.VMEM((tokens, rows), jnp.float32),
+            pltpu.VMEM(w_value.shape, jnp.bfloat16),
+        ],
+        in_specs=[anywhere] * 8,
+        out_specs=[on_chip] * 4,
         scratch_shapes=[
+            pltpu.SMEM(block_order.shape, jnp.int32),
+            pltpu.VMEM((1, latent_width), jnp.float32),
             pltpu.VMEM(query_nope.shape, jnp.bfloat16),
             pltpu.VMEM(query_rope.shape, jnp.bfloat16),
             pltpu.VMEM(w_key.shape, jnp.bfloat16),
-            pltpu.VMEM(w_value.shape, jnp.bfloat16),
             pltpu.VMEM((contexts, shards) + kv_latent.shape, jnp.bfloat16),
             pltpu.VMEM((contexts, shards, rope_rows, ROPE), jnp.bfloat16),
-            pltpu.VMEM((heads * tokens, latent_width + LANES), jnp.bfloat16),
-            pltpu.VMEM((contexts * tokens, latent_width + LANES), jnp.bfloat16),
-            pltpu.VMEM((tokens, heads * VALUE_DIM), jnp.bfloat16),
             pltpu.SemaphoreType.DMA((3,)),
             pltpu.SemaphoreType.DMA((4,)),
-            pltpu.SemaphoreType.DMA((2,)),
-            pltpu.SemaphoreType.DMA((heads // HEAD_GROUP,)),
+            pltpu.SemaphoreType.DMA((4,)),
             pltpu.SemaphoreType.DMA((sends,)),
             pltpu.SemaphoreType.DMA((contexts, shards)),
             pltpu.SemaphoreType.DMA((sends,)),
             pltpu.SemaphoreType.DMA((contexts, shards)),
         ],
-        compiler_params=pltpu.CompilerParams(collective_id=0, has_side_effects=True),
+        compiler_params=pltpu.CompilerParams(
+            collective_id=0,
+            has_side_effects=True,
+            vmem_limit_bytes=VMEM_BYTES - VMEM_SPARE - handed,
+        ),
     )(
         block_order,
         latent_gain.reshape(1, latent_width),
@@ -526,6 +546,17 @@
         w_key,
         w_value,
     )
+    return pl.pallas_call(
+        attend_kernel,
+        out_shape=jax.ShapeDtypeStruct((tokens, heads * VALUE_DIM), jnp.bfloat16),
+        in_specs=[on_chip] * 4,
+        out_specs=anywhere,
+        scratch_shapes=[
+            pltpu.VMEM((tokens, heads * VALUE_DIM), jnp.bfloat16),
+            pltpu.SemaphoreType.DMA((heads // HEAD_GROUP,)),
+        ],
+        compiler_params=pltpu.CompilerParams(vmem_limit_bytes=VMEM_GRANT),
+    )(*prepared)
 
 
 def power_of_two(count):

time: 19.3 us -> 16.5 us (0.85)
  local copies, waits for them, and re-layouts: 1.67 us -> 0 us
  Pallas kernels: 17.5 us -> 16.3 us
    unnamed x1 -> x0, local copies, waits for them, and re-layouts: 1.67 us -> none
    pallas_call x1 -> x2, Pallas kernels: 17.5 us -> 16.3 us  [the longest x1 13.1 us: fused_device(): pl.pallas_call(partial(fused_kernel, contexts, shards), out_shape=[pltpu....]
where the time goes in v2:
time: 16.5 us; the launch traced here: 16.3 us
  Pallas kernels  16.3 us (99%)
    pallas_call x1, Pallas kernels, fused_device(): pl.pallas_call(partial(fused_kernel, contexts, shards), out_shape=[pltpu....  13.1 us
    pallas_call x1, Pallas kernels, fused_device(): pl.pallas_call(attend_kernel, out_shape=jax.ShapeDtypeStruct((tokens, hea...  3.23 us

profile of v2, /device:TPU:1, one launch (start us, length us, event | category | flops | bytes accessed | tf_op | source)
XLA Modules:
  0.0 16.3 jit_solution(10703087263632563707)
XLA Ops:
  0.0 13.1 %shard_map.82 = (bf16[1024,640]{1,0:T(8,128)(2,1)S(1)}, bf16[256,640]{1,0:T(8,128)(2,1)S(1)}, f32[64,256]{1,0:T(8,128)S(1)}, bf16[512,2048]{1,0:T(8,128)(2,1)S(1)}) custom-call(s32[8]{0:T(128)} %order_hbm.1, f32[1,512]{1,0:T(1,128)} %bitcast.1, bf16[64,2048]{1,0:T(8,128)(2,1)} %nope_hbm.1, bf16[64,1024]{1,0:T(8,128)(2,1)} %rope_hbm.1, ...), custom_call_target="tpu_custom_call" | custom-call | tf_op jit(solution)/shard_map/pallas_call | solution.py:508
  13.1 3.2 %shard_map.83 = bf16[64,2048]{1,0:T(8,128)(2,1)} custom-call(bf16[1024,640]{1,0:T(8,128)(2,1)S(1)} %get-tuple-element.9.queries, bf16[256,640]{1,0:T(8,128)(2,1)S(1)} %get-tuple-element.10.keys, f32[64,256]{1,0:T(8,128)S(1)} %get-tuple-element.11.bias, bf16[512,2048]{1,0:T(8,128)(2,1)S(1)} %get-tuple-element.12.w_value), custom_call_target="tpu_custom_call" | custom-call | tf_op jit(solution)/shard_map/pallas_call | solution.py:549
